TPU v7x, 32 devices: a whole 2x2x4 slice. The times are simulated.
32 devices in a mesh: path: 16 (over z, x, core), shard: 2 (over y).
Axes of the slice: x: 2, y: 2, z: 4, core: 2. Of those that a mesh axis runs over, the one named last changes fastest.
Arguments:
- deltas: bfloat16 [16, 32, 4096], P('path', 'shard'), may hold values from -96 to 96
- momentum: float32 [16, 32, 4096], P(None, 'shard', 'path'), may hold values from -4 to 4
- path_module: int32 [16], replicated, may hold values from 0 to 15, as said below
Outputs:
- path_update: bfloat16 [16, 32, 4096], P('path', 'shard')
- new_momentum: float32 [16, 32, 4096], P(None, 'shard', 'path')
Inputs may be any that keep to these rules, and one draw needn't show every extreme that they name: `path_module`: every module is used by at least one and at most seven paths.
All inputs are finite; a program needn't handle non-finite values.
Results may differ from a plain program's by a relative error of at most 0.0004.
Values may be sent and summed in bfloat16 or wider, within the bound.
A program may use at most 64 MiB of HBM per device.

v0:
```python
import jax
import jax.numpy as jnp
from jax import lax
from jax.sharding import PartitionSpec as P

D = 4096


outer_rate = 0.7
momentum_rate = 0.9
clip_ratio = 2.0


def local(deltas, momentum, path_module):
    own_index = lax.axis_index("path")
    modules = momentum.shape[0]
    row_count = deltas.shape[1]
    onehot = (path_module[:, None] == jnp.arange(modules, dtype=jnp.int32)[None, :]).astype(
        jnp.float32
    )
    counts = jnp.sum(onehot, axis=0)
    own_module = lax.dynamic_index_in_dim(path_module, own_index, 0, keepdims=False)
    column_pieces = lax.all_to_all(deltas, "path", split_axis=2, concat_axis=0, tiled=True)
    totals = jnp.einsum(
        "pm,prc->mrc",
        onehot.astype(jnp.bfloat16),
        column_pieces,
        preferred_element_type=jnp.float32,
    )
    outer_grad = totals / counts[:, None, None]
    local_squares = jnp.sum(outer_grad * outer_grad, axis=(1, 2))
    norm_squares = lax.psum(local_squares, ("path", "shard"))
    limit = clip_ratio * jnp.sqrt(jnp.float32(row_count * lax.axis_size("shard") * D))
    shrink = jnp.minimum(1.0, limit / jnp.sqrt(norm_squares + 1e-06))
    clipped = outer_grad * shrink[:, None, None]
    new_momentum = momentum_rate * momentum + clipped
    outer_step = (outer_rate * (clipped + momentum_rate * new_momentum)).astype(jnp.bfloat16)
    gathered = lax.all_gather(outer_step, "path", axis=2, tiled=True)
    path_update = lax.dynamic_index_in_dim(gathered, own_module, 0, keepdims=True)
    return (path_update, new_momentum)


def solution(mesh):
    return jax.shard_map(
        local,
        mesh=mesh,
        in_specs=(P("path", "shard", None), P(None, "shard", "path"), P()),
        out_specs=(P("path", "shard", None), P(None, "shard", "path")),
        check_vma=False,
    )
```

profile of v0, /device:TPU:0, one launch (start us, length us, event | category | flops | bytes accessed | tf_op | source)
XLA Modules:
  0.0 145.2 jit_solution(7055501070345371449)
XLA Ops:
  7.2 4.3 %copy.8 = bf16[1,16,4096]{1,0,2:T(2,128)(2,1)S(1)} copy(bf16[1,16,4096]{2,1,0:T(8,128)(2,1)} %param.3) | data formatting | bytes 262144 | tf_op args[0]
  11.5 0.5 broadcast.26
  12.0 0.0 copy-start.1
  12.0 22.4 %reduce = bf16[4096,16]{1,0:T(8,128)(2,1)S(1)} reduce(bf16[4096,1,16]{2,1,0:T(2,128)(2,1)S(1)} %bitcast.25, bf16[]{:T(256)} %broadcast.26), dimensions={1}, to_apply=%bitcast.15.reduce_sub_computation | reduce | bytes 262146
  34.4 1.8 %reshape.8 = bf16[16,2,2048]{2,1,0:T(2,128)(2,1)} reshape(bf16[4096,16]{1,0:T(8,128)(2,1)S(1)} %reduce) | data formatting | bytes 262144
  36.2 7.4 %all-to-all-start = ((bf16[16,2,2048]{2,1,0:T(2,128)(2,1)}), bf16[16,2,2048]{2,1,0:T(2,128)(2,1)S(1)}, u32[]{:S(2)}, u32[]{:S(2)}) async-start(bf16[16,2,2048]{2,1,0:T(2,128)(2,1)} %reshape.8), calls=%async_computation | async-start | bytes 262144 | tf_op jit(solution)/shard_map/all_to_all | solution.py:23
  43.6 0.0 all-gather.2.cloned.1.call-start
  43.6 0.0 copy-done.1
  43.6 0.1 convert_reduce_fusion
  43.8 7.7 %all-to-all-done = bf16[16,2,2048]{2,1,0:T(2,128)(2,1)S(1)} async-done(((bf16[16,2,2048]{2,1,0:T(2,128)(2,1)}), bf16[16,2,2048]{2,1,0:T(2,128)(2,1)S(1)}, u32[]{:S(2)}, u32[]{:S(2)}) %all-to-all-start) | async-done | bytes 131104 | tf_op jit(solution)/shard_map/all_to_all | solution.py:23
  51.5 1.8 %reshape.9 = bf16[4096,1,16]{2,1,0:T(2,128)(2,1)S(1)} reshape(bf16[16,2,2048]{2,1,0:T(2,128)(2,1)S(1)} %all-to-all-done) | data formatting | bytes 262144
  53.3 0.0 copy-start
  53.3 2.0 %copy.9 = bf16[1,16,4096]{2,1,0:T(8,128)(2,1)S(1)} copy(bf16[1,16,4096]{1,0,2:T(2,128)(2,1)S(1)} %bitcast.26) | data formatting | bytes 262144 | tf_op jit(solution)/shard_map/all_to_all | solution.py:23
  55.3 0.3 multiply_reduce_fusion
  55.6 37.5 %psum.7 = f32[16]{0:T(128)S(1)} all-reduce(f32[16]{0:T(128)S(1)} %get-tuple-element.8), channel_id=1, replica_groups=mesh['path'=16,'shard'=2] {'path','shard'}, use_global_device_ids=true, to_apply=%region_2.3 | all-reduce | flops 16 | bytes 128 | tf_op jit(solution)/shard_map/psum | solution.py:32
  93.1 0.0 copy-done
  93.1 0.9 fusion
  94.0 0.0 all-gather.2.cloned.1.call-update
  94.0 0.6 dynamic_slice.8
  96.5 0.9 copy.12
  97.4 38.6 %all-gather.2.cloned.1.call-done = bf16[16,16,4096]{2,0,1:T(8,128)(2,1)} async-done(((bf16[16,16,256]{2,0,1:T(8,128)(2,1)}), bf16[16,16,4096]{2,0,1:T(8,128)(2,1)}) %all-gather.2.cloned.1.call-update) | async-done | bytes 2097168 | tf_op jit(solution)/shard_map/all_gather | solution.py:38
  136.0 1.5 %constant_dynamic-slice_fusion = bf16[1,16,4096]{2,0,1:T(2,128)(2,1)S(1)} fusion(bf16[16,16,4096]{2,0,1:T(8,128)(2,1)} %all-gather.2.cloned.1.call-done, s32[]{:T(128)S(6)} %select_n.9), kind=kLoop, calls=%fused_computation.12 | loop fusion | bytes 262148 | tf_op jit(solution)/shard_map/jit(dynamic_index_in_dim)/dynamic_slice | solution.py:39
  137.5 0.8 copy.11
  (2 shorter events, 0.0 us)
Async XLA Ops:
  12.0 31.6 %copy-start.1 = (s32[16]{0:T(128)S(1)}, s32[16]{0:T(128)}, u32[]{:S(2)}) copy-start(s32[16]{0:T(128)} %param.5) | copy-start | bytes 196
  36.2 15.3 %all-to-all-start = ((bf16[16,2,2048]{2,1,0:T(2,128)(2,1)}), bf16[16,2,2048]{2,1,0:T(2,128)(2,1)S(1)}, u32[]{:S(2)}, u32[]{:S(2)}) async-start(bf16[16,2,2048]{2,1,0:T(2,128)(2,1)} %reshape.8), calls=%async_computation | async-start | bytes 262144 | tf_op jit(solution)/shard_map/all_to_all | solution.py:23
  43.6 92.4 %all-gather.2.cloned.1.call-start = ((), (), s32[]{:S(2)}) async-start(), calls=%async_computation.1 | async-start | bytes 2228224 | tf_op jit(solution)/shard_map/all_gather | solution.py:38
  53.3 39.8 %copy-start = (f32[16,16,256]{2,1,0:T(8,128)S(1)}, f32[16,16,256]{2,1,0:T(8,128)}, u32[]{:S(2)}) copy-start(f32[16,16,256]{2,1,0:T(8,128)} %param.4) | copy-start | bytes 786436
Sparse Core Ops, SparseCore 0:
  94.1 41.7 all-gather.1
where the time goes:
time: 146 us; the launch traced here: 145 us
  waiting for transfers between devices  46.3 us (32%)
  blocking collectives  37.5 us (26%)
  other arithmetic  23.4 us (16%)
  between operations  16 us (11%)
  local copies, waits for them, and re-layouts  14.2 us (10%)
  starting transfers between devices  7.43 us (5%)
    all_gather x1, waiting for transfers between devices, local(): gathered = lax.all_gather(outer_step, 'path', axis=2, tiled=True)  38.6 us
    psum x1, blocking collectives, local(): norm_squares = lax.psum(local_squares, ('path', 'shard'))  37.5 us
    unnamed x1, other arithmetic  22.4 us
    unnamed x11, local copies, waits for them, and re-layouts  10.1 us
    all_to_all x1, waiting for transfers between devices, local(): lax.all_to_all(deltas, 'path', split_axis=2, concat_axis=0, tiled=True)  7.73 us
    all_to_all x1, starting transfers between devices, local(): lax.all_to_all(deltas, 'path', split_axis=2, concat_axis=0, tiled=True)  7.39 us
  transfers between devices with their start and end apart: 2, of which 2 were waited for; matrix products, arithmetic and copies ran while one was open for 1% of the time, Pallas kernels for 0%

commit v1 on v0

v1 whole, which is shorter than its diff:
```python
import functools
import math

import jax
import jax.numpy as jnp
from jax import lax
from jax.experimental import pallas as pl
from jax.experimental.pallas import tpu as pltpu
from jax.sharding import PartitionSpec as P

outer_rate = 0.7
momentum_rate = 0.9
clip_ratio = 2.0
LANES = 128
MESH = pl.DeviceIdType.MESH


def kernel(
    n,
    s,
    deltas_ref,
    momentum_ref,
    module_ref,
    update_ref,
    new_ref,
    own,
    pieces,
    momentum,
    grad,
    new,
    step,
    chosen,
    squares,
    load_sem,
    local_sem,
    send_sem,
    recv_sem,
    square_send,
    square_recv,
    back_send,
    back_recv,
):
    me, my_shard = lax.axis_index("path"), lax.axis_index("shard")
    modules, rows, columns = momentum.shape
    width = own.shape[1]
    everyone = [(k, j) for k in range(n) for j in range(s) if (k, j) != (0, 0)]

    def peer(k, j=0):
        return lax.rem(me + k, n), lax.rem(my_shard + j, s)

    def device(k, j=0):
        there, shard = peer(k, j)
        return {"path": there, "shard": shard}

    def block(index):
        return pl.ds(pl.multiple_of(index * columns, columns), columns)

    load_own = pltpu.make_async_copy(deltas_ref.at[0], own, load_sem.at[0])
    load_own.start()
    load_momentum = pltpu.make_async_copy(momentum_ref, momentum, load_sem.at[1])
    load_momentum.start()
    barrier = pltpu.get_barrier_semaphore()
    for k, j in everyone:
        pl.semaphore_signal(barrier, inc=1, device_id=device(k, j), device_id_type=MESH)

    lane = lax.broadcasted_iota(jnp.int32, (1, n * rows), 1)
    target = jnp.zeros((1, n * rows), jnp.int32)
    for p in range(n):
        inside = (lane >= p * rows) & (lane < (p + 1) * rows)
        target = jnp.where(inside, lane + (module_ref[p] - p) * rows, target)
    row = lax.broadcasted_iota(jnp.int32, (modules * rows, n * rows), 0)
    spread = (row == target).astype(jnp.float32)
    scale = 1.0 / jnp.sum(spread, axis=1, keepdims=True)
    spread = spread.astype(jnp.bfloat16)

    load_own.wait()
    keep_own = pltpu.make_async_copy(own.at[:, block(me)], pieces.at[me], local_sem.at[0])
    keep_own.start()
    pl.semaphore_wait(barrier, len(everyone))
    sends = []
    for k in range(1, n):
        there, _ = peer(k)
        copy = pltpu.make_async_remote_copy(
            src_ref=own.at[:, block(there)],
            dst_ref=pieces.at[me],
            send_sem=send_sem.at[k],
            recv_sem=recv_sem.at[k],
            device_id=device(k),
            device_id_type=MESH,
        )
        copy.start()
        sends.append(copy)
    keep_own.wait()
    for copy in sends:
        copy.wait_recv()

    total = jnp.dot(
        spread, pieces[...].reshape(n * rows, columns), preferred_element_type=jnp.float32
    )
    outer_grad = (total * scale).reshape(modules, rows, columns)
    grad[...] = outer_grad
    by_row = jnp.sum(outer_grad * outer_grad, axis=1)
    by_module = jnp.sum(by_row, axis=1, keepdims=True)
    on_diagonal = lax.broadcasted_iota(
        jnp.int32, (modules, LANES), 0
    ) == lax.broadcasted_iota(jnp.int32, (modules, LANES), 1)
    own_squares = jnp.sum(jnp.where(on_diagonal, by_module, 0.0), axis=0, keepdims=True)
    my_slot = me * s + my_shard
    squares[my_slot] = own_squares
    square_copies = []
    for at, (k, j) in enumerate(everyone):
        copy = pltpu.make_async_remote_copy(
            src_ref=squares.at[my_slot],
            dst_ref=squares.at[my_slot],
            send_sem=square_send.at[at],
            recv_sem=square_recv.at[at],
            device_id=device(k, j),
            device_id_type=MESH,
        )
        copy.start()
        square_copies.append(copy)
    load_momentum.wait()
    for copy in square_copies:
        copy.wait_recv()
    norm_squares = jnp.sum(squares[...], axis=0)
    limit = clip_ratio * math.sqrt(rows * s * width)
    shrink = jnp.minimum(1.0, limit / jnp.sqrt(norm_squares + 1e-06))
    at_lane = lax.broadcasted_iota(jnp.int32, (1, LANES), 1)
    for m in range(modules):
        factor = jnp.sum(jnp.where(at_lane == m, shrink, 0.0), axis=1, keepdims=True)
        clipped = grad[m] * factor
        moved = momentum_rate * momentum[m] + clipped
        new[m] = moved
        step[m] = (outer_rate * (clipped + momentum_rate * moved)).astype(jnp.bfloat16)
    for p in range(n):
        chosen[p] = step[module_ref[p]]
    returns = []
    for k in range(1, n):
        there, _ = peer(k)
        copy = pltpu.make_async_remote_copy(
            src_ref=chosen.at[there],
            dst_ref=update_ref.at[0, :, block(me)],
            send_sem=back_send.at[k],
            recv_sem=back_recv.at[k],
            device_id=device(k),
            device_id_type=MESH,
        )
        copy.start()
        returns.append(copy)
    put_own = pltpu.make_async_copy(
        chosen.at[me], update_ref.at[0, :, block(me)], local_sem.at[1]
    )
    put_own.start()
    put_new = pltpu.make_async_copy(new, new_ref, local_sem.at[2])
    put_new.start()
    for copy in sends + square_copies:
        copy.wait_send()
    put_own.wait()
    put_new.wait()
    for copy in returns:
        copy.wait()


def direct(n, s, deltas, momentum, path_module):
    modules, rows, columns = momentum.shape
    width = deltas.shape[2]
    dma = pltpu.SemaphoreType.DMA
    anywhere = pl.BlockSpec(memory_space=pl.ANY)
    return pl.pallas_call(
        functools.partial(kernel, n, s),
        out_shape=(
            jax.ShapeDtypeStruct(deltas.shape, jnp.bfloat16),
            jax.ShapeDtypeStruct(momentum.shape, jnp.float32),
        ),
        in_specs=[anywhere, anywhere, pl.BlockSpec(memory_space=pltpu.SMEM)],
        out_specs=(anywhere, anywhere),
        scratch_shapes=[
            pltpu.VMEM((rows, width), jnp.bfloat16),
            pltpu.VMEM((n, rows, columns), jnp.bfloat16),
            pltpu.VMEM((modules, rows, columns), jnp.float32),
            pltpu.VMEM((modules, rows, columns), jnp.float32),
            pltpu.VMEM((modules, rows, columns), jnp.float32),
            pltpu.VMEM((modules, rows, columns), jnp.bfloat16),
            pltpu.VMEM((n, rows, columns), jnp.bfloat16),
            pltpu.VMEM((n * s, 1, LANES), jnp.float32),
            dma((2,)),
            dma((3,)),
            dma((n,)),
            dma((n,)),
            dma((n * s,)),
            dma((n * s,)),
            dma((n,)),
            dma((n,)),
        ],
        compiler_params=pltpu.CompilerParams(collective_id=0, has_side_effects=True),
    )(deltas, momentum, path_module)


def by_collectives(s, deltas, momentum, path_module):
    modules = momentum.shape[0]
    rows, width = deltas.shape[1:]
    onehot = path_module[:, None] == jnp.arange(modules, dtype=jnp.int32)[None, :]
    counts = jnp.sum(onehot.astype(jnp.float32), axis=0)
    pieces = lax.all_to_all(deltas, "path", split_axis=2, concat_axis=0, tiled=True)
    totals = jnp.einsum(
        "pm,prc->mrc", onehot.astype(jnp.bfloat16), pieces, preferred_element_type=jnp.float32
    )
    outer_grad = totals / counts[:, None, None]
    local_squares = jnp.sum(outer_grad * outer_grad, axis=(1, 2))
    norm_squares = lax.psum(local_squares, ("path", "shard"))
    limit = clip_ratio * math.sqrt(rows * s * width)
    shrink = jnp.minimum(1.0, limit / jnp.sqrt(norm_squares + 1e-06))
    clipped = outer_grad * shrink[:, None, None]
    new_momentum = momentum_rate * momentum + clipped
    outer_step = (outer_rate * (clipped + momentum_rate * new_momentum)).astype(jnp.bfloat16)
    chosen = jnp.take(outer_step, path_module, axis=0)
    path_update = lax.all_to_all(chosen, "path", split_axis=0, concat_axis=2, tiled=True)
    return (path_update, new_momentum)


def local(n, s, deltas, momentum, path_module):
    modules, rows, columns = momentum.shape
    aligned = columns % LANES == 0 and rows % 16 == 0 and modules <= LANES
    if aligned and n > 1:
        return direct(n, s, deltas, momentum, path_module)
    return by_collectives(s, deltas, momentum, path_module)


def solution(mesh):
    return jax.shard_map(
        functools.partial(local, mesh.shape["path"], mesh.shape["shard"]),
        mesh=mesh,
        in_specs=(P("path", "shard", None), P(None, "shard", "path"), P()),
        out_specs=(P("path", "shard", None), P(None, "shard", "path")),
        check_vma=False,
    )
```

time: 146 us -> 24.7 us (0.17)
  waiting for transfers between devices: 46.3 us -> 0 us
  blocking collectives: 37.5 us -> 0 us
  other arithmetic: 23.4 us -> 0 us
  Pallas kernels: 0 us -> 21.5 us
  between operations: 16 us -> 0.65 us
  local copies, waits for them, and re-layouts: 14.2 us -> 2.32 us
  starting transfers between devices: 7.43 us -> 0 us
    all_gather x1 -> x0, waiting for transfers between devices: 38.6 us -> none  [local(): gathered = lax.all_gather(outer_step, 'path', axis=2, tiled=True)]
    psum x1 -> x0, blocking collectives: 37.5 us -> none  [local(): norm_squares = lax.psum(local_squares, ('path', 'shard'))]
    unnamed x1 -> x0, other arithmetic: 22.4 us -> none
    pallas_call x0 -> x1, Pallas kernels: none -> 21.5 us  [direct(): pl.pallas_call(functools.partial(kernel, n, s), out_shape=(jax.ShapeDtype...]
    unnamed x11 -> x4, local copies, waits for them, and re-layouts: 10.1 us -> 2.32 us
    all_to_all x1 -> x0, waiting for transfers between devices: 7.73 us -> none  [local(): lax.all_to_all(deltas, 'path', split_axis=2, concat_axis=0, tiled=True)]
    all_to_all x1 -> x0, starting transfers between devices: 7.39 us -> none  [local(): lax.all_to_all(deltas, 'path', split_axis=2, concat_axis=0, tiled=True)]
    dynamic_slice x2 -> x0, local copies, waits for them, and re-layouts: 2.12 us -> none  [the longest x1 1.53 us: local(): lax.dynamic_index_in_dim(gathered, own_module, 0, keepdims=True)]
  transfers between devices with their start and end apart: 2 -> 0, of which waited for: 2 -> 0; matrix products, arithmetic and copies ran while one was open for 1% -> 0% of each run, Pallas kernels for 0% -> 0%
where the time goes in v1:
time: 24.7 us; the launch traced here: 24.5 us
  Pallas kernels  21.5 us (87%)
  local copies, waits for them, and re-layouts  2.32 us (9%)
  between operations  0.65 us (3%)
    pallas_call x1, Pallas kernels, direct(): pl.pallas_call(functools.partial(kernel, n, s), out_shape=(jax.ShapeDtype...  21.5 us
    unnamed x4, local copies, waits for them, and re-layouts  2.32 us

profile of v1, /device:TPU:0, one launch (start us, length us, event | category | flops | bytes accessed | tf_op | source)
XLA Modules:
  0.0 24.5 jit_solution(6721259658559049352)
XLA Ops:
  0.6 21.5 %shard_map.50 = (bf16[1,16,4096]{2,1,0:T(8,128)(2,1)}, f32[16,16,256]{2,1,0:T(8,128)}) custom-call(bf16[1,16,4096]{2,1,0:T(8,128)(2,1)} %deltas_ref.1, f32[16,16,256]{2,1,0:T(8,128)} %momentum_ref.1, s32[16]{0:T(128)} %module_ref.1), custom_call_target="tpu_custom_call" | custom-call | tf_op jit(solution)/shard_map/pallas_call | solution.py:169
  22.1 0.0 copy-start
  22.1 1.6 %copy.7 = bf16[1,16,4096]{2,1,0:T(8,128)(2,1)} copy(bf16[1,16,4096]{2,1,0:T(8,128)(2,1)} %get-tuple-element.4) | data formatting | bytes 262144
  23.8 0.0 copy-done
  23.8 0.7 %copy.8 = f32[16,16,256]{2,1,0:T(8,128)} copy(f32[16,16,256]{2,1,0:T(8,128)S(1)} %copy-done) | data formatting | bytes 524288
Async XLA Ops:
  22.1 1.6 %copy-start = (f32[16,16,256]{2,1,0:T(8,128)S(1)}, f32[16,16,256]{2,1,0:T(8,128)}, u32[]{:S(2)}) copy-start(f32[16,16,256]{2,1,0:T(8,128)} %get-tuple-element.5) | copy-start | bytes 786436

commit v2 on v1

--- a/solution.py
+++ b/solution.py
@@ -20,19 +20,19 @@
     s,
     deltas_ref,
     momentum_ref,
+    path_module_ref,
+    update,
+    new,
     module_ref,
-    update_ref,
-    new_ref,
     own,
     pieces,
     momentum,
     grad,
-    new,
     step,
     chosen,
+    mine,
     squares,
     load_sem,
-    local_sem,
     send_sem,
     recv_sem,
     square_send,
@@ -52,16 +52,22 @@
         there, shard = peer(k, j)
         return {"path": there, "shard": shard}
 
+    def arrived(buffer, sem):
+        pltpu.make_async_copy(buffer, buffer, sem).wait()
+
     def block(index):
         return pl.ds(pl.multiple_of(index * columns, columns), columns)
 
+    barrier = pltpu.get_barrier_semaphore()
+    for k, j in everyone:
+        pl.semaphore_signal(barrier, inc=1, device_id=device(k, j), device_id_type=MESH)
+    load_module = pltpu.make_async_copy(path_module_ref, module_ref, load_sem.at[2])
+    load_module.start()
     load_own = pltpu.make_async_copy(deltas_ref.at[0], own, load_sem.at[0])
     load_own.start()
     load_momentum = pltpu.make_async_copy(momentum_ref, momentum, load_sem.at[1])
     load_momentum.start()
-    barrier = pltpu.get_barrier_semaphore()
-    for k, j in everyone:
-        pl.semaphore_signal(barrier, inc=1, device_id=device(k, j), device_id_type=MESH)
+    load_module.wait()
 
     lane = lax.broadcasted_iota(jnp.int32, (1, n * rows), 1)
     target = jnp.zeros((1, n * rows), jnp.int32)
@@ -74,25 +80,21 @@
     spread = spread.astype(jnp.bfloat16)
 
     load_own.wait()
-    keep_own = pltpu.make_async_copy(own.at[:, block(me)], pieces.at[me], local_sem.at[0])
+    keep_own = pltpu.make_async_copy(own.at[:, block(me)], pieces.at[me], recv_sem)
     keep_own.start()
     pl.semaphore_wait(barrier, len(everyone))
-    sends = []
     for k in range(1, n):
         there, _ = peer(k)
         copy = pltpu.make_async_remote_copy(
             src_ref=own.at[:, block(there)],
             dst_ref=pieces.at[me],
-            send_sem=send_sem.at[k],
-            recv_sem=recv_sem.at[k],
+            send_sem=send_sem,
+            recv_sem=recv_sem,
             device_id=device(k),
             device_id_type=MESH,
         )
         copy.start()
-        sends.append(copy)
-    keep_own.wait()
-    for copy in sends:
-        copy.wait_recv()
+    arrived(pieces, recv_sem)
 
     total = jnp.dot(
         spread, pieces[...].reshape(n * rows, columns), preferred_element_type=jnp.float32
@@ -106,22 +108,20 @@
     ) == lax.broadcasted_iota(jnp.int32, (modules, LANES), 1)
     own_squares = jnp.sum(jnp.where(on_diagonal, by_module, 0.0), axis=0, keepdims=True)
     my_slot = me * s + my_shard
-    squares[my_slot] = own_squares
-    square_copies = []
-    for at, (k, j) in enumerate(everyone):
+    mine[...] = own_squares
+    for k, j in everyone:
         copy = pltpu.make_async_remote_copy(
-            src_ref=squares.at[my_slot],
+            src_ref=mine,
             dst_ref=squares.at[my_slot],
-            send_sem=square_send.at[at],
-            recv_sem=square_recv.at[at],
+            send_sem=square_send,
+            recv_sem=square_recv,
             device_id=device(k, j),
             device_id_type=MESH,
         )
         copy.start()
-        square_copies.append(copy)
+    pltpu.make_async_copy(mine, squares.at[my_slot], square_recv).start()
     load_momentum.wait()
-    for copy in square_copies:
-        copy.wait_recv()
+    arrived(squares, square_recv)
     norm_squares = jnp.sum(squares[...], axis=0)
     limit = clip_ratio * math.sqrt(rows * s * width)
     shrink = jnp.minimum(1.0, limit / jnp.sqrt(norm_squares + 1e-06))
@@ -134,30 +134,34 @@
         step[m] = (outer_rate * (clipped + momentum_rate * moved)).astype(jnp.bfloat16)
     for p in range(n):
         chosen[p] = step[module_ref[p]]
-    returns = []
     for k in range(1, n):
         there, _ = peer(k)
         copy = pltpu.make_async_remote_copy(
             src_ref=chosen.at[there],
-            dst_ref=update_ref.at[0, :, block(me)],
-            send_sem=back_send.at[k],
-            recv_sem=back_recv.at[k],
+            dst_ref=update.at[0, :, block(me)],
+            send_sem=back_send,
+            recv_sem=back_recv,
             device_id=device(k),
             device_id_type=MESH,
         )
         copy.start()
-        returns.append(copy)
-    put_own = pltpu.make_async_copy(
-        chosen.at[me], update_ref.at[0, :, block(me)], local_sem.at[1]
-    )
-    put_own.start()
-    put_new = pltpu.make_async_copy(new, new_ref, local_sem.at[2])
-    put_new.start()
-    for copy in sends + square_copies:
-        copy.wait_send()
-    put_own.wait()
-    put_new.wait()
-    for copy in returns:
+    pltpu.make_async_copy(
+        chosen.at[me], update.at[0, :, block(me)], back_recv
+    ).start()
+    arrived(pieces.at[pl.ds(0, n - 1)], send_sem)
+    arrived(squares.at[pl.ds(0, len(everyone))], square_send)
+    arrived(chosen.at[pl.ds(0, n - 1)], back_send)
+    arrived(update, back_recv)
+
+
+def write(update, new, update_ref, new_ref, sem):
+    copies = [
+        pltpu.make_async_copy(update, update_ref, sem.at[0]),
+        pltpu.make_async_copy(new, new_ref, sem.at[1]),
+    ]
+    for copy in copies:
+        copy.start()
+    for copy in copies:
         copy.wait()
 
 
@@ -166,34 +170,45 @@
     width = deltas.shape[2]
     dma = pltpu.SemaphoreType.DMA
     anywhere = pl.BlockSpec(memory_space=pl.ANY)
+    in_vmem = pl.BlockSpec(memory_space=pltpu.VMEM)
+    held = pl.pallas_call(
+        functools.partial(kernel, n, s),
+        out_shape=(
+            pltpu.VMEM(deltas.shape, jnp.bfloat16),
+            pltpu.VMEM(momentum.shape, jnp.float32),
+        ),
+        in_specs=[anywhere, anywhere, anywhere],
+        out_specs=(in_vmem, in_vmem),
+        scratch_shapes=[
+            pltpu.SMEM(path_module.shape, jnp.int32),
+            pltpu.VMEM((rows, width), jnp.bfloat16),
+            pltpu.VMEM((n, rows, columns), jnp.bfloat16),
+            pltpu.VMEM((modules, rows, columns), jnp.float32),
+            pltpu.VMEM((modules, rows, columns), jnp.float32),
+            pltpu.VMEM((modules, rows, columns), jnp.bfloat16),
+            pltpu.VMEM((n, rows, columns), jnp.bfloat16),
+            pltpu.VMEM((1, LANES), jnp.float32),
+            pltpu.VMEM((n * s, 1, LANES), jnp.float32),
+            dma((3,)),
+            dma,
+            dma,
+            dma,
+            dma,
+            dma,
+            dma,
+        ],
+        compiler_params=pltpu.CompilerParams(collective_id=0, has_side_effects=True),
+    )(deltas, momentum, path_module)
     return pl.pallas_call(
-        functools.partial(kernel, n, s),
+        write,
         out_shape=(
             jax.ShapeDtypeStruct(deltas.shape, jnp.bfloat16),
             jax.ShapeDtypeStruct(momentum.shape, jnp.float32),
         ),
-        in_specs=[anywhere, anywhere, pl.BlockSpec(memory_space=pltpu.SMEM)],
+        in_specs=[in_vmem, in_vmem],
         out_specs=(anywhere, anywhere),
-        scratch_shapes=[
-            pltpu.VMEM((rows, width), jnp.bfloat16),
-            pltpu.VMEM((n, rows, columns), jnp.bfloat16),
-            pltpu.VMEM((modules, rows, columns), jnp.float32),
-            pltpu.VMEM((modules, rows, columns), jnp.float32),
-            pltpu.VMEM((modules, rows, columns), jnp.float32),
-            pltpu.VMEM((modules, rows, columns), jnp.bfloat16),
-            pltpu.VMEM((n, rows, columns), jnp.bfloat16),
-            pltpu.VMEM((n * s, 1, LANES), jnp.float32),
-            dma((2,)),
-            dma((3,)),
-            dma((n,)),
-            dma((n,)),
-            dma((n * s,)),
-            dma((n * s,)),
-            dma((n,)),
-            dma((n,)),
-        ],
-        compiler_params=pltpu.CompilerParams(collective_id=0, has_side_effects=True),
-    )(deltas, momentum, path_module)
+        scratch_shapes=[dma((2,))],
+    )(*[pltpu.with_memory_space_constraint(x, pltpu.VMEM) for x in held])
 
 
 def by_collectives(s, deltas, momentum, path_module):

time: 24.7 us -> 21.2 us (0.86)
  local copies, waits for them, and re-layouts: 2.32 us -> 0 us
  Pallas kernels: 21.5 us -> 20.3 us
    unnamed x4 -> x0, local copies, waits for them, and re-layouts: 2.32 us -> none
    pallas_call x1 -> x2, Pallas kernels: 21.5 us -> 20.3 us  [the longest x1 19.5 us: direct(): pl.pallas_call(functools.partial(kernel, n, s), out_shape=(pltpu.VMEM(del...]
where the time goes in v2:
time: 21.2 us; the launch traced here: 20.9 us
  Pallas kernels  20.3 us (96%)
  between operations  0.64 us (3%)
    pallas_call x1, Pallas kernels, direct(): pl.pallas_call(functools.partial(kernel, n, s), out_shape=(pltpu.VMEM(del...  19.5 us
    pallas_call x1, Pallas kernels, direct(): pl.pallas_call(write, out_shape=(jax.ShapeDtypeStruct(deltas.shape, jnp.b...  0.77 us

profile of v2, /device:TPU:0, one launch (start us, length us, event | category | flops | bytes accessed | tf_op | source)
XLA Modules:
  0.0 20.9 jit_solution(3734097839343791157)
XLA Ops:
  0.6 19.5 %shard_map.50 = (bf16[1,16,4096]{2,1,0:T(8,128)(2,1)S(1)}, f32[16,16,256]{2,1,0:T(8,128)S(1)}) custom-call(bf16[1,16,4096]{2,1,0:T(8,128)(2,1)} %deltas_ref.1, f32[16,16,256]{2,1,0:T(8,128)} %momentum_ref.1, s32[16]{0:T(128)} %path_module_ref.1), custom_call_target="tpu_custom_call" | custom-call | tf_op jit(solution)/shard_map/pallas_call | solution.py:174
  20.2 0.8 %shard_map.51 = (bf16[1,16,4096]{2,1,0:T(8,128)(2,1)}, f32[16,16,256]{2,1,0:T(8,128)}) custom-call(bf16[1,16,4096]{2,1,0:T(8,128)(2,1)S(1)} %get-tuple-element.4.update, f32[16,16,256]{2,1,0:T(8,128)S(1)} %get-tuple-element.5.new), custom_call_target="tpu_custom_call" | custom-call | tf_op jit(solution)/shard_map/pallas_call | solution.py:202

commit v3 on v2

--- a/solution.py
+++ b/solution.py
@@ -46,7 +46,8 @@
     everyone = [(k, j) for k in range(n) for j in range(s) if (k, j) != (0, 0)]
 
     def peer(k, j=0):
-        return lax.rem(me + k, n), lax.rem(my_shard + j, s)
+        there, shard = me + k, my_shard + j
+        return jnp.where(there < n, there, there - n), jnp.where(shard < s, shard, shard - s)
 
     def device(k, j=0):
         there, shard = peer(k, j)
@@ -54,6 +55,20 @@
 
     def arrived(buffer, sem):
         pltpu.make_async_copy(buffer, buffer, sem).wait()
+
+    def targets():
+        size = math.gcd(n, 4)
+        groups = n // size
+        group, place = me // size, lax.rem(me, size)
+        low = group < groups // 2
+        for a in range(groups):
+            down, up = groups - 1 - a, a
+            down = jnp.where(down <= group, down - 1, down)
+            up = jnp.where(up >= group, up + 1, up)
+            other = group if a == groups - 1 else jnp.where(low, down, up)
+            for b in range(1 if a == groups - 1 else 0, size):
+                at = place + b
+                yield other * size + jnp.where(at < size, at, at - size)
 
     def block(index):
         return pl.ds(pl.multiple_of(index * columns, columns), columns)
@@ -83,14 +98,13 @@
     keep_own = pltpu.make_async_copy(own.at[:, block(me)], pieces.at[me], recv_sem)
     keep_own.start()
     pl.semaphore_wait(barrier, len(everyone))
-    for k in range(1, n):
-        there, _ = peer(k)
+    for there in targets():
         copy = pltpu.make_async_remote_copy(
             src_ref=own.at[:, block(there)],
             dst_ref=pieces.at[me],
             send_sem=send_sem,
             recv_sem=recv_sem,
-            device_id=device(k),
+            device_id={"path": there, "shard": my_shard},
             device_id_type=MESH,
         )
         copy.start()
@@ -132,10 +146,10 @@
         moved = momentum_rate * momentum[m] + clipped
         new[m] = moved
         step[m] = (outer_rate * (clipped + momentum_rate * moved)).astype(jnp.bfloat16)
-    for p in range(n):
-        chosen[p] = step[module_ref[p]]
+    chosen[me] = step[module_ref[me]]
     for k in range(1, n):
         there, _ = peer(k)
+        chosen[there] = step[module_ref[there]]
         copy = pltpu.make_async_remote_copy(
             src_ref=chosen.at[there],
             dst_ref=update.at[0, :, block(me)],

time: 21.2 us -> 21.1 us (level)
  no operation moved by 1% of the time
where the time goes in v3:
time: 21.1 us; the launch traced here: 21 us
  Pallas kernels  20.3 us (96%)
  between operations  0.64 us (3%)
    pallas_call x1, Pallas kernels, direct(): pl.pallas_call(functools.partial(kernel, n, s), out_shape=(pltpu.VMEM(del...  19.6 us
    pallas_call x1, Pallas kernels, direct(): pl.pallas_call(write, out_shape=(jax.ShapeDtypeStruct(deltas.shape, jnp.b...  0.77 us

profile of v3, /device:TPU:0, one launch (start us, length us, event | category | flops | bytes accessed | tf_op | source)
XLA Modules:
  0.0 21.0 jit_solution(7073615365743450334)
XLA Ops:
  0.6 19.6 %shard_map.50 = (bf16[1,16,4096]{2,1,0:T(8,128)(2,1)S(1)}, f32[16,16,256]{2,1,0:T(8,128)S(1)}) custom-call(bf16[1,16,4096]{2,1,0:T(8,128)(2,1)} %deltas_ref.1, f32[16,16,256]{2,1,0:T(8,128)} %momentum_ref.1, s32[16]{0:T(128)} %path_module_ref.1), custom_call_target="tpu_custom_call" | custom-call | tf_op jit(solution)/shard_map/pallas_call | solution.py:188
  20.2 0.8 %shard_map.51 = (bf16[1,16,4096]{2,1,0:T(8,128)(2,1)}, f32[16,16,256]{2,1,0:T(8,128)}) custom-call(bf16[1,16,4096]{2,1,0:T(8,128)(2,1)S(1)} %get-tuple-element.4.update, f32[16,16,256]{2,1,0:T(8,128)S(1)} %get-tuple-element.5.new), custom_call_target="tpu_custom_call" | custom-call | tf_op jit(solution)/shard_map/pallas_call | solution.py:216
